TPU v7x, 32 devices: a whole 2x2x4 slice. The times are simulated.
32 devices in a mesh: row: 8 (over z, y), col: 4 (over x, core).
Axes of the slice: x: 2, y: 2, z: 4, core: 2. Of those that a mesh axis runs over, the one named last changes fastest.
Arguments:
- layer_input: bfloat16 [2048, 8192], P('row'), may hold values from -7 to 7
- gain: float32 [8192], replicated, may hold values from 0.5 to 6
- d_query: bfloat16 [2048, 4096], P('row', 'col'), may hold values from -6 to 6
- d_keyval: bfloat16 [2048, 2048], P('row', 'col'), may hold values from -6 to 6
- w_query: bfloat16 [8192, 4096], P('row', 'col'), may hold values from -0.0625 to 0.0625
- w_keyval: bfloat16 [8192, 2048], P('row', 'col'), may hold values from -1 to 1
- d_resid: bfloat16 [2048, 8192], P('row', 'col'), may hold values from -6 to 6
Outputs:
- d_input: bfloat16 [2048, 8192], P('row', 'col')
- grad_wq: bfloat16 [8192, 4096], P('row', 'col')
- grad_wkv: bfloat16 [8192, 2048], P('row', 'col')
- grad_gain: float32 [8192], P('col')
- grad_square_sum: float32 [], replicated
All inputs are finite; a program needn't handle non-finite values.
Results may differ from a plain program's by a relative error of at most 0.023.
Values may be sent and summed in bfloat16 or wider, within the bound.
A program may use at most 128 MiB of HBM per device.

v0:
```python
import math
import jax
import jax.numpy as jnp
from jax import lax
from jax.sharding import PartitionSpec as P

epsilon = 1e-05


def local(layer_input, gain, d_query, d_keyval, w_query, w_keyval, d_resid):
    inputs = layer_input.astype(jnp.float32)
    inv_rms = lax.rsqrt(jnp.mean(inputs * inputs, axis=1, keepdims=True) + epsilon)
    normed = (inputs * inv_rms * gain).astype(jnp.bfloat16)
    model_width = inputs.shape[1]
    local_tokens = inputs.shape[0]
    tokens_all = local_tokens * lax.axis_size("row")
    scaling = 1.0 / math.sqrt(tokens_all)
    weight_scale = 1.0 / math.sqrt(local_tokens)
    contract_cols = (((1,), (1,)), ((), ()))
    query_cols = d_query.shape[1]
    cotangent = jnp.concatenate([d_query, d_keyval], axis=1)
    all_cotangents = lax.all_gather(cotangent, "row", axis=0, tiled=True)
    weights = jnp.concatenate([w_query, w_keyval], axis=1)
    partial_value = lax.dot_general(
        all_cotangents, weights, contract_cols, preferred_element_type=jnp.float32
    )
    reduced = lax.psum_scatter(
        partial_value.astype(jnp.bfloat16), "col", scatter_dimension=0, tiled=True
    )
    n_row, n_col = (lax.axis_size("row"), lax.axis_size("col"))
    fold = n_row // n_col
    pieces = reduced.reshape(fold, local_tokens, reduced.shape[1])
    row, col = (lax.axis_index("row"), lax.axis_index("col"))
    arrived = []
    for shift in range(fold):
        pairs = [
            (r * n_col + c, (fold * c + (r + shift) % fold) * n_col + r // fold)
            for r in range(n_row)
            for c in range(n_col)
        ]
        piece = lax.dynamic_index_in_dim(pieces, (row + shift) % fold, 0, keepdims=False)
        arrived.append(lax.ppermute(piece, ("row", "col"), pairs))
    arrived = jnp.stack(arrived)
    feature_grad = jnp.concatenate(
        [
            lax.dynamic_index_in_dim(arrived, (row - j + fold) % fold, 0, keepdims=False)
            for j in range(fold)
        ],
        axis=1,
    ).astype(jnp.float32)
    slice_width = feature_grad.shape[1]
    col_start = lax.axis_index("col") * slice_width
    input_part = lax.dynamic_slice_in_dim(inputs, col_start, slice_width, 1)
    gain_part = lax.dynamic_slice_in_dim(gain, col_start, slice_width, 0)
    weighted = gain_part * feature_grad
    token_dot = lax.psum(jnp.sum(weighted * input_part, axis=1, keepdims=True), "col")
    d_input = (
        d_resid.astype(jnp.float32)
        + inv_rms * weighted
        - input_part * inv_rms**3 * token_dot / model_width
    ).astype(jnp.bfloat16)
    gain_partial = jnp.sum(feature_grad * input_part * inv_rms, axis=0) * scaling
    cotangent = jnp.concatenate([d_query, d_keyval], axis=1)
    columns = lax.all_to_all(normed, "row", split_axis=1, concat_axis=0, tiled=True)
    groups = lax.axis_size("row")
    column_blocks = columns.reshape(groups, local_tokens, columns.shape[1])
    grad_blocks = all_cotangents.reshape(groups, local_tokens, all_cotangents.shape[1])
    blocks = (
        lax.dot_general(
            column_blocks,
            grad_blocks,
            (((1,), (1,)), ((0,), (0,))),
            preferred_element_type=jnp.float32,
        )
        * weight_scale
    )
    summed = jnp.sum(blocks.astype(jnp.bfloat16).astype(jnp.float32), axis=0)
    grad_wq = summed[:, :query_cols].astype(jnp.bfloat16)
    grad_wkv = summed[:, query_cols:].astype(jnp.bfloat16)
    query_f = grad_wq.astype(jnp.float32)
    keyval_f = grad_wkv.astype(jnp.float32)
    tile_square = jnp.sum(query_f * query_f) + jnp.sum(keyval_f * keyval_f)
    grad_gain = lax.psum(gain_partial, "row")
    leading = jnp.where(
        lax.axis_index("row") == 0, jnp.sum(grad_gain * grad_gain), jnp.float32(0.0)
    )
    grand_total = lax.psum(tile_square + leading, ("row", "col"))
    grad_square_sum = grand_total / jnp.float32(model_width)
    return (d_input, grad_wq, grad_wkv, grad_gain, grad_square_sum)


def solution(mesh):
    placed = (
        P("row", None),
        P(),
        P("row", "col"),
        P("row", "col"),
        P("row", "col"),
        P("row", "col"),
        P("row", "col"),
    )
    return jax.shard_map(
        local,
        mesh=mesh,
        in_specs=placed,
        out_specs=(P("row", "col"), P("row", "col"), P("row", "col"), P("col"), P()),
        check_vma=False,
    )
```

profile of v0, /device:TPU:13, one launch (start us, length us, event | category | flops | bytes accessed | tf_op | source)
XLA Modules:
  0.0 376.0 jit_solution(1316032979656445743)
XLA Ops:
  7.2 2.1 pad_maximum_fusion.1
  9.3 3.3 multiply_reduce_fusion
  12.6 0.2 copy-done
  12.8 3.1 multiply_convert_fusion.1
  15.9 6.5 %copy.12 = bf16[256,8192]{0,1:T(8,128)(2,1)} copy(bf16[256,8192]{1,0:T(8,128)(2,1)} %multiply_convert_fusion.1) | data formatting | bytes 8388608 | tf_op jit(solution)/shard_map/convert_element_type | solution.py:13
  22.3 5.8 %all-to-all-start = ((bf16[256,8,1024]{0,2,1:T(8,128)(2,1)}), bf16[256,8,1024]{0,2,1:T(8,128)(2,1)}, u32[]{:S(2)}, u32[]{:S(2)}) async-start(bf16[256,8,1024]{0,2,1:T(8,128)(2,1)} %bitcast.18), calls=%async_computation.1 | async-start | bytes 8388608 | tf_op jit(solution)/shard_map/all_to_all | solution.py:64
  28.1 150.8 %all-gather.2.cloned.1.call-done = bf16[2048,1536]{1,0:T(8,128)(2,1)} async-done(((bf16[256,1536]{1,0:T(8,128)(2,1)}), bf16[2048,1536]{1,0:T(8,128)(2,1)}) %all-gather.2.cloned.1.call-update) | async-done | bytes 6291472 | tf_op jit(solution)/shard_map/all_gather | solution.py:22
  179.0 10.4 %convolution_convert_fusion = bf16[2048,1024]{1,0:T(8,128)(2,1)} fusion(bf16[2048,1536]{1,0:T(8,128)(2,1)} %all-gather.2.cloned.1.call-done, bf16[1024,512]{1,0:T(8,128)(2,1)} %param.12, bf16[1024,1024]{1,0:T(8,128)(2,1)S(1)} %copy-done.4), kind=kOutput, calls=%fused_computation.6 | convolution fusion | flops 6450839552 | bytes 13631488 | tf_op jit(solution)/shard_map/dot_general | solution.py:24
  189.5 6.4 %convert_element_type.33 = f32[256,8192]{1,0:T(8,128)} convert(bf16[256,8192]{1,0:T(8,128)(2,1)} %param.7) | non-fusion elementwise | flops 2097152 | bytes 12582912 | tf_op jit(solution)/shard_map/convert_element_type | solution.py:11
  195.9 10.9 %fusion = bf16[1024,1536]{1,0:T(8,128)(2,1)S(1)} fusion(bf16[8,256,1536]{2,1,0:T(8,128)(2,1)} %bitcast.20, bf16[256,8,1024]{0,2,1:T(8,128)(2,1)} %all-to-all-done), kind=kOutput, calls=%fused_computation.3 | convolution fusion | flops 6478626816 | bytes 13631488 | tf_op jit(solution)/shard_map/dot_general | solution.py:69
  206.8 36.0 %reduce-scatter.2.cloned.1.call-done = bf16[512,1024]{1,0:T(8,128)(2,1)} async-done(((bf16[2048,1024]{1,0:T(8,128)(2,1)}), bf16[512,1024]{1,0:T(8,128)(2,1)}) %reduce-scatter.2.cloned.1.call-update) | async-done | bytes 1048592 | tf_op jit(solution)/shard_map/reduce_scatter | solution.py:27
  242.8 2.3 dynamic-slice_bitcast_fusion
  245.1 0.3 collective-permute-start.1
  245.3 5.3 %collective-permute-start = (bf16[256,1024]{1,0:T(8,128)(2,1)}, bf16[256,1024]{1,0:T(8,128)(2,1)}, u32[]{:S(2)}, u32[]{:S(2)}) collective-permute-start(bf16[256,1024]{1,0:T(8,128)(2,1)} %get-tuple-element.14), channel_id=1, source_target_pairs={{0,0},{1,8},{2,16},{3,24},{4,4},{5,12},{6,20},{7,28},{8,1},{9,9},{... | collective-permute-start | bytes 1572872 | tf_op jit(solution)/shard_map/ppermute | solution.py:42
  250.7 2.0 multiply_reduce_fusion.2
  252.7 2.9 multiply_reduce_fusion.1
  257.1 2.3 collective-permute-done.1
  259.3 1.6 fusion.16
  260.9 2.2 fusion.12
  263.2 47.4 %psum.22 = f32[2048]{0:T(1024)S(1)} all-reduce(f32[2048]{0:T(1024)S(1)} %broadcast_multiply_fusion), channel_id=1, replica_groups=mesh['row'=8,'col'=4] {'row'}, use_global_device_ids=true, to_apply=%region_6.7 | all-reduce | flops 2048 | bytes 16384 | tf_op jit(solution)/shard_map/psum | solution.py:83
  310.5 0.6 multiply_reduce_fusion.3
  311.8 45.0 %psum.23 = f32[]{:T(128)} all-reduce(f32[]{:T(128)S(6)} %add.80), channel_id=1, replica_groups=mesh['row'=8,'col'=4] {'row','col'}, use_global_device_ids=true, to_apply=%region_10.11 | all-reduce | flops 1 | bytes 8 | tf_op jit(solution)/shard_map/psum | solution.py:87
  356.8 7.3 %psum.21 = f32[256]{0:T(256)S(1)} all-reduce(f32[256]{0:T(256)S(1)} %get-tuple-element.6), channel_id=1, replica_groups=mesh['row'=8,'col'=4] {'col'}, use_global_device_ids=true, to_apply=%region_3.4 | all-reduce | flops 256 | bytes 2048 | tf_op jit(solution)/shard_map/psum | solution.py:56
  364.8 3.3 fusion.9
  (18 shorter events, 0.1 us)
Async XLA Ops:
  7.2 5.4 %copy-start.2 = (f32[8192]{0:T(1024)S(1)}, f32[8192]{0:T(1024)}, u32[]{:S(2)}) copy-start(f32[8192]{0:T(1024)} %param.8) | copy-start | bytes 98308
  7.2 171.8 %all-gather.2.cloned.1.call-start = ((), (), s32[]{:S(2)}) async-start(), calls=%async_computation.2 | async-start | bytes 7077888 | tf_op jit(solution)/shard_map/all_gather | solution.py:22
  9.3 3.5 copy-start
  22.3 156.6 %copy-start.4 = (bf16[1024,1024]{1,0:T(8,128)(2,1)S(1)}, bf16[1024,1024]{1,0:T(8,128)(2,1)}, u32[]{:S(2)}) copy-start(bf16[1024,1024]{1,0:T(8,128)(2,1)} %param.11) | copy-start | bytes 6291460
  22.3 173.5 %all-to-all-start = ((bf16[256,8,1024]{0,2,1:T(8,128)(2,1)}), bf16[256,8,1024]{0,2,1:T(8,128)(2,1)}, u32[]{:S(2)}, u32[]{:S(2)}) async-start(bf16[256,8,1024]{0,2,1:T(8,128)(2,1)} %bitcast.18), calls=%async_computation.1 | async-start | bytes 8388608 | tf_op jit(solution)/shard_map/all_to_all | solution.py:64
  28.1 214.7 %reduce-scatter.2.cloned.1.call-start = ((), (), s32[]{:S(2)}) async-start(), calls=%async_computation.3 | async-start | bytes 5242880 | tf_op jit(solution)/shard_map/reduce_scatter | solution.py:27
  245.1 14.3 %collective-permute-start.1 = (bf16[256,1024]{1,0:T(8,128)(2,1)}, bf16[256,1024]{1,0:T(8,128)(2,1)}, u32[]{:S(2)}, u32[]{:S(2)}) collective-permute-start(bf16[256,1024]{1,0:T(8,128)(2,1)} %get-tuple-element.13), channel_id=1, source_target_pairs={{0,4},{1,12},{2,20},{3,28},{4,0},{5,8},{6,16},{7,24},{8,5},{9,13},... | collective-permute-start | bytes 1572872 | tf_op jit(solution)/shard_map/ppermute | solution.py:42
  245.3 14.0 %collective-permute-start = (bf16[256,1024]{1,0:T(8,128)(2,1)}, bf16[256,1024]{1,0:T(8,128)(2,1)}, u32[]{:S(2)}, u32[]{:S(2)}) collective-permute-start(bf16[256,1024]{1,0:T(8,128)(2,1)} %get-tuple-element.14), channel_id=1, source_target_pairs={{0,0},{1,8},{2,16},{3,24},{4,4},{5,12},{6,20},{7,28},{8,1},{9,9},{... | collective-permute-start | bytes 1572872 | tf_op jit(solution)/shard_map/ppermute | solution.py:42
  255.7 109.1 %copy-start.1 = (bf16[256,2048]{1,0:T(8,128)(2,1)S(1)}, bf16[256,2048]{1,0:T(8,128)(2,1)}, u32[]{:S(2)}) copy-start(bf16[256,2048]{1,0:T(8,128)(2,1)} %param.13) | copy-start | bytes 3145732
  310.5 57.5 %copy-start.3 = (f32[2048]{0:T(1024)}, f32[2048]{0:T(1024)S(1)}, u32[]{:S(2)}) copy-start(f32[2048]{0:T(1024)S(1)} %psum.22) | copy-start | bytes 24580
Sparse Core Ops, SparseCore 0:
  10.7 168.1 all-gather.1
  189.5 53.2 reduce-scatter.1
where the time goes:
time: 377 us; the launch traced here: 376 us
  waiting for transfers between devices  189 us (50%)
  blocking collectives  99.7 us (26%)
  other arithmetic  27.5 us (7%)
  matrix products  21.3 us (6%)
  between operations  18 us (5%)
  starting transfers between devices  11.4 us (3%)
  local copies, waits for them, and re-layouts  8.96 us (2%)
    all_gather x1, waiting for transfers between devices, local(): all_cotangents = lax.all_gather(cotangent, 'row', axis=0, tiled=True)  151 us
    psum x1, blocking collectives, local(): grad_gain = lax.psum(gain_partial, 'row')  47.4 us
    psum x1, blocking collectives, local(): grand_total = lax.psum(tile_square + leading, ('row', 'col'))  45 us
    reduce_scatter x1, waiting for transfers between devices, local(): lax.psum_scatter(partial_value.astype(jnp.bfloat16), 'col', scatter_dimen...  36 us
    dot_general x1, matrix products, local(): lax.dot_general(column_blocks, grad_blocks, (((1,), (1,)), ((0,), (0,))),...  10.9 us
    dot_general x1, matrix products, local(): lax.dot_general(all_cotangents, weights, contract_cols, preferred_element...  10.4 us
  transfers between devices with their start and end apart: 5, of which 3 were waited for; matrix products, arithmetic and copies ran while one was open for 12% of the time, Pallas kernels for 0%

commit v1 on v0

--- a/solution.py
+++ b/solution.py
@@ -1,3 +1,4 @@
+import functools
 import math
 import jax
 import jax.numpy as jnp
@@ -5,6 +6,20 @@
 from jax.sharding import PartitionSpec as P
 
 epsilon = 1e-05
+
+
+def follow_the_signs(slab_in, named_axis):
+    size_here = lax.axis_size(named_axis)
+    o_now = lambda block_now: [(q, q ^ block_now) for q in range(size_here)]
+    local_next = slab_in
+    for hop_no in range(size_here.bit_length() - 1):
+        res = o_now(1 << hop_no)
+        upper = lax.ppermute(local_next, named_axis, res)
+        local_next = local_next + upper
+    return local_next
+
+
+task_register = functools.partial(follow_the_signs, named_axis="row")
 
 
 def local(layer_input, gain, d_query, d_keyval, w_query, w_keyval, d_resid):
@@ -80,7 +95,7 @@
     query_f = grad_wq.astype(jnp.float32)
     keyval_f = grad_wkv.astype(jnp.float32)
     tile_square = jnp.sum(query_f * query_f) + jnp.sum(keyval_f * keyval_f)
-    grad_gain = lax.psum(gain_partial, "row")
+    grad_gain = task_register(gain_partial)
     leading = jnp.where(
         lax.axis_index("row") == 0, jnp.sum(grad_gain * grad_gain), jnp.float32(0.0)
     )

time: 377 us -> 365 us (0.968)
  blocking collectives: 99.7 us -> 45.1 us
  starting transfers between devices: 11.4 us -> 55.7 us
  waiting for transfers between devices: 189 us -> 182 us
    all_gather x1, waiting for transfers between devices: 151 us -> 97.9 us  [local(): all_cotangents = lax.all_gather(cotangent, 'row', axis=0, tiled=True)]
    all_to_all x1, waiting for transfers between devices: 0.01 us -> 51.9 us  [local(): lax.all_to_all(normed, 'row', split_axis=1, concat_axis=0, tiled=True)]
    ppermute x0 -> x3, starting transfers between devices: none -> 47.8 us  [follow_the_signs(): upper = lax.ppermute(local_next, named_axis, res)]
    psum x1 -> x0, blocking collectives: 47.4 us -> none  [local(): grad_gain = lax.psum(gain_partial, 'row')]
    reduce_scatter x1, waiting for transfers between devices: 36 us -> 26.1 us  [local(): lax.psum_scatter(partial_value.astype(jnp.bfloat16), 'col', scatter_dimen...]
    psum x1, blocking collectives: 45 us -> 40 us  [local(): grand_total = lax.psum(tile_square + leading, ('row', 'col'))]
    ppermute x2, starting transfers between devices: 5.61 us -> 1.21 us  [local(): arrived.append(lax.ppermute(piece, ('row', 'col'), pairs))]
  transfers between devices with their start and end apart: 5 -> 8, of which waited for: 3 -> 4; matrix products, arithmetic and copies ran while one was open for 12% -> 12% of each run, Pallas kernels for 0% -> 0%
where the time goes in v1:
time: 365 us; the launch traced here: 362 us
  waiting for transfers between devices  182 us (50%)
  starting transfers between devices  55.7 us (15%)
  blocking collectives  45.1 us (12%)
  other arithmetic  30 us (8%)
  matrix products  23.8 us (7%)
  between operations  17.9 us (5%)
  local copies, waits for them, and re-layouts  8.13 us (2%)
    all_gather x1, waiting for transfers between devices, local(): all_cotangents = lax.all_gather(cotangent, 'row', axis=0, tiled=True)  97.9 us
    all_to_all x1, waiting for transfers between devices, local(): lax.all_to_all(normed, 'row', split_axis=1, concat_axis=0, tiled=True)  51.9 us
    ppermute x3, starting transfers between devices, follow_the_signs(): upper = lax.ppermute(local_next, named_axis, res)  47.8 us
    psum x1, blocking collectives, local(): grand_total = lax.psum(tile_square + leading, ('row', 'col'))  40 us
    reduce_scatter x1, waiting for transfers between devices, local(): lax.psum_scatter(partial_value.astype(jnp.bfloat16), 'col', scatter_dimen...  26.1 us
    dot_general x1, matrix products, local(): lax.dot_general(column_blocks, grad_blocks, (((1,), (1,)), ((0,), (0,))),...  12.6 us
    dot_general x1, matrix products, local(): lax.dot_general(all_cotangents, weights, contract_cols, preferred_element...  11.1 us
    reduce_sum x2, other arithmetic, local(): tile_square = jnp.sum(query_f * query_f) + jnp.sum(keyval_f * keyval_f)  7.8 us
  transfers between devices with their start and end apart: 8, of which 4 were waited for; matrix products, arithmetic and copies ran while one was open for 12% of the time, Pallas kernels for 0%

profile of v1, /device:TPU:13, one launch (start us, length us, event | category | flops | bytes accessed | tf_op | source)
XLA Modules:
  0.0 362.5 jit_solution(15004594802166053011)
XLA Ops:
  7.2 2.1 pad_maximum_fusion.1
  9.3 97.9 %all-gather.2.cloned.1.call-done = bf16[2048,1536]{1,0:T(8,128)(2,1)} async-done(((bf16[256,1536]{1,0:T(8,128)(2,1)}), bf16[2048,1536]{1,0:T(8,128)(2,1)}) %all-gather.2.cloned.1.call-update) | async-done | bytes 6291472 | tf_op jit(solution)/shard_map/all_gather | solution.py:37
  107.2 11.1 %convolution_convert_fusion = bf16[2048,1024]{1,0:T(8,128)(2,1)} fusion(bf16[2048,1536]{1,0:T(8,128)(2,1)} %all-gather.2.cloned.1.call-done, bf16[1024,512]{1,0:T(8,128)(2,1)} %param.12, bf16[1024,1024]{1,0:T(8,128)(2,1)} %param.11), kind=kOutput, calls=%fused_computation.6 | convolution fusion | flops 6450839552 | bytes 13631488 | tf_op jit(solution)/shard_map/dot_general | solution.py:39
  118.4 3.3 multiply_reduce_fusion
  121.9 3.2 multiply_convert_fusion.1
  125.1 6.7 %copy.12 = bf16[256,8192]{0,1:T(8,128)(2,1)} copy(bf16[256,8192]{1,0:T(8,128)(2,1)} %multiply_convert_fusion.1) | data formatting | bytes 8388608 | tf_op jit(solution)/shard_map/convert_element_type | solution.py:28
  131.8 6.6 %all-to-all-start = ((bf16[256,8,1024]{0,2,1:T(8,128)(2,1)}), bf16[256,8,1024]{0,2,1:T(8,128)(2,1)}, u32[]{:S(2)}, u32[]{:S(2)}) async-start(bf16[256,8,1024]{0,2,1:T(8,128)(2,1)} %bitcast.18), calls=%async_computation.1 | async-start | bytes 8388608 | tf_op jit(solution)/shard_map/all_to_all | solution.py:79
  138.3 26.1 %reduce-scatter.2.cloned.1.call-done = bf16[512,1024]{1,0:T(8,128)(2,1)} async-done(((bf16[2048,1024]{1,0:T(8,128)(2,1)}), bf16[512,1024]{1,0:T(8,128)(2,1)}) %reduce-scatter.2.cloned.1.call-update) | async-done | bytes 1048592 | tf_op jit(solution)/shard_map/reduce_scatter | solution.py:42
  164.5 1.3 dynamic-slice_bitcast_fusion
  166.1 0.9 collective-permute-start
  167.0 6.5 %convert_element_type.33 = f32[256,8192]{1,0:T(8,128)} convert(bf16[256,8192]{1,0:T(8,128)(2,1)} %param.7) | non-fusion elementwise | flops 2097152 | bytes 12582912 | tf_op jit(solution)/shard_map/convert_element_type | solution.py:26
  173.5 6.0 %collective-permute-done.1 = bf16[256,1024]{1,0:T(8,128)(2,1)S(1)} collective-permute-done((bf16[256,1024]{1,0:T(8,128)(2,1)S(1)}, bf16[256,1024]{1,0:T(8,128)(2,1)S(1)}, u32[]{:S(2)}, u32[]{:S(2)}) %collective-permute-start.1) | collective-permute-done | bytes 524320 | tf_op jit(solution)/shard_map/ppermute | solution.py:57
  179.5 0.4 fusion.16
  179.9 2.2 fusion.12
  182.2 51.9 %all-to-all-done = bf16[256,8,1024]{0,2,1:T(8,128)(2,1)} async-done(((bf16[256,8,1024]{0,2,1:T(8,128)(2,1)}), bf16[256,8,1024]{0,2,1:T(8,128)(2,1)}, u32[]{:S(2)}, u32[]{:S(2)}) %all-to-all-start) | async-done | bytes 4194336 | tf_op jit(solution)/shard_map/all_to_all | solution.py:79
  234.1 12.6 %fusion = bf16[1024,1536]{1,0:T(8,128)(2,1)} fusion(bf16[8,256,1536]{2,1,0:T(8,128)(2,1)} %bitcast.22, bf16[256,8,1024]{0,2,1:T(8,128)(2,1)} %all-to-all-done), kind=kOutput, calls=%fused_computation.3 | convolution fusion | flops 6478626816 | bytes 13631488 | tf_op jit(solution)/shard_map/dot_general | solution.py:84
  246.7 19.6 %collective-permute-start.3 = (f32[2048]{0:T(1024)S(1)}, f32[2048]{0:T(1024)S(1)}, u32[]{:S(2)}, u32[]{:S(2)}) collective-permute-start(f32[2048]{0:T(1024)S(1)} %fusion.18), channel_id=1, source_target_pairs={{0,8},{4,12},{8,0},{12,4},{16,24},{20,28},{24,16},{28,20},{1,9},{5... | collective-permute-start | bytes 24584 | tf_op jit(solution)/shard_map/ppermute | solution.py:17
  266.3 4.5 %multiply_reduce_fusion.1 = (f32[]{:T(128)}, bf16[1024,1024]{1,0:T(8,128)(2,1)}) fusion(bf16[1024,1536]{1,0:T(8,128)(2,1)} %fusion), kind=kLoop, calls=%fused_computation.5 | loop fusion | flops 3145727 | bytes 4194308 | tf_op jit(solution)/shard_map/reduce_sum | solution.py:97
  270.9 28.1 %collective-permute-start.4 = (f32[2048]{0:T(1024)S(1)}, f32[2048]{0:T(1024)S(1)}, u32[]{:S(2)}, u32[]{:S(2)}) collective-permute-start(f32[2048]{0:T(1024)S(1)} %add.87), channel_id=1, source_target_pairs={{0,16},{4,20},{8,24},{12,28},{16,0},{20,4},{24,8},{28,12},{1,17},{... | collective-permute-start | bytes 24584 | tf_op jit(solution)/shard_map/ppermute | solution.py:17
  299.0 3.3 multiply_reduce_fusion.2
  303.6 5.1 %psum.14 = f32[256]{0:T(256)S(1)} all-reduce(f32[256]{0:T(256)S(1)} %get-tuple-element.6), channel_id=1, replica_groups=mesh['row'=8,'col'=4] {'col'}, use_global_device_ids=true, to_apply=%region_3.4 | all-reduce | flops 256 | bytes 2048 | tf_op jit(solution)/shard_map/psum | solution.py:71
  308.7 1.2 multiply_reduce_fusion.3
  310.6 3.3 fusion.9
  313.8 40.0 %psum.15 = f32[]{:T(128)} all-reduce(f32[]{:T(128)S(6)} %add.90), channel_id=1, replica_groups=mesh['row'=8,'col'=4] {'row','col'}, use_global_device_ids=true, to_apply=%region_9.10 | all-reduce | flops 1 | bytes 8 | tf_op jit(solution)/shard_map/psum | solution.py:102
  (21 shorter events, 0.7 us)
Async XLA Ops:
  7.2 100.1 %all-gather.2.cloned.1.call-start = ((), (), s32[]{:S(2)}) async-start(), calls=%async_computation.2 | async-start | bytes 7077888 | tf_op jit(solution)/shard_map/all_gather | solution.py:37
  9.3 155.2 %reduce-scatter.2.cloned.1.call-start = ((), (), s32[]{:S(2)}) async-start(), calls=%async_computation.3 | async-start | bytes 5242880 | tf_op jit(solution)/shard_map/reduce_scatter | solution.py:42
  118.4 3.3 copy-start.2
  118.4 3.5 copy-start
  131.8 102.3 %all-to-all-start = ((bf16[256,8,1024]{0,2,1:T(8,128)(2,1)}), bf16[256,8,1024]{0,2,1:T(8,128)(2,1)}, u32[]{:S(2)}, u32[]{:S(2)}) async-start(bf16[256,8,1024]{0,2,1:T(8,128)(2,1)} %bitcast.18), calls=%async_computation.1 | async-start | bytes 8388608 | tf_op jit(solution)/shard_map/all_to_all | solution.py:79
  165.7 13.7 %collective-permute-start.1 = (bf16[256,1024]{1,0:T(8,128)(2,1)S(1)}, bf16[256,1024]{1,0:T(8,128)(2,1)S(1)}, u32[]{:S(2)}, u32[]{:S(2)}) collective-permute-start(bf16[256,1024]{1,0:T(8,128)(2,1)S(1)} %get-tuple-element.15), channel_id=1, source_target_pairs={{0,4},{1,12},{2,20},{3,28},{4,0},{5,8},{6,16},{7,24},{8,5},{9,13},... | collective-permute-start | bytes 1572872 | tf_op jit(solution)/shard_map/ppermute | solution.py:57
  166.1 13.4 %collective-permute-start = (bf16[256,1024]{1,0:T(8,128)(2,1)S(1)}, bf16[256,1024]{1,0:T(8,128)(2,1)S(1)}, u32[]{:S(2)}, u32[]{:S(2)}) collective-permute-start(bf16[256,1024]{1,0:T(8,128)(2,1)S(1)} %get-tuple-element.16), channel_id=1, source_target_pairs={{0,0},{1,8},{2,16},{3,24},{4,4},{5,12},{6,20},{7,28},{8,1},{9,9},{... | collective-permute-start | bytes 1572872 | tf_op jit(solution)/shard_map/ppermute | solution.py:57
  182.1 64.6 %collective-permute-start.2 = (f32[2048]{0:T(1024)S(1)}, f32[2048]{0:T(1024)S(1)}, u32[]{:S(2)}, u32[]{:S(2)}) collective-permute-start(f32[2048]{0:T(1024)S(1)} %broadcast_multiply_fusion), channel_id=1, source_target_pairs={{0,4},{4,0},{8,12},{12,8},{16,20},{20,16},{24,28},{28,24},{1,5},{5... | collective-permute-start | bytes 24584 | tf_op jit(solution)/shard_map/ppermute | solution.py:17
  246.7 63.8 %copy-start.1 = (bf16[256,2048]{1,0:T(8,128)(2,1)S(1)}, bf16[256,2048]{1,0:T(8,128)(2,1)}, u32[]{:S(2)}) copy-start(bf16[256,2048]{1,0:T(8,128)(2,1)} %param.13) | copy-start | bytes 3145732
  246.7 24.2 %collective-permute-start.3 = (f32[2048]{0:T(1024)S(1)}, f32[2048]{0:T(1024)S(1)}, u32[]{:S(2)}, u32[]{:S(2)}) collective-permute-start(f32[2048]{0:T(1024)S(1)} %fusion.18), channel_id=1, source_target_pairs={{0,8},{4,12},{8,0},{12,4},{16,24},{20,28},{24,16},{28,20},{1,9},{5... | collective-permute-start | bytes 24584 | tf_op jit(solution)/shard_map/ppermute | solution.py:17
  270.9 37.8 %collective-permute-start.4 = (f32[2048]{0:T(1024)S(1)}, f32[2048]{0:T(1024)S(1)}, u32[]{:S(2)}, u32[]{:S(2)}) collective-permute-start(f32[2048]{0:T(1024)S(1)} %add.87), channel_id=1, source_target_pairs={{0,16},{4,20},{8,24},{12,28},{16,0},{20,4},{24,8},{28,12},{1,17},{... | collective-permute-start | bytes 24584 | tf_op jit(solution)/shard_map/ppermute | solution.py:17
Sparse Core Ops, SparseCore 0:
  10.7 96.4 all-gather.1
  118.5 45.9 reduce-scatter.1
